TPU v7x, 32 devices: a whole 2x2x4 slice. The times are simulated.
32 devices in a mesh: section: 2 (over x), lat: 4 (over z), lon: 4 (over y, core).
Axes of the slice: x: 2, y: 2, z: 4, core: 2. Of those that a mesh axis runs over, the one named last changes fastest.
Arguments:
- state: bfloat16 [2, 112, 360, 1024], P('section', 'lat', 'lon'), may hold values from -6 to 6
- fresh: bfloat16 [112, 360, 1024], P('lat', 'lon'), may hold values from -6 to 6
- cutoff: int32 [3], replicated, may hold values from 0 to 15
- plan: int32 [2, 2], replicated, may hold values from 0 to 1
- lmax: int32 [2], replicated, may hold values from 56 to 112, as said below
- mmax: int32 [2], replicated, may hold values from 24 to 96, as said below
- cutoff_table: float32 [16, 1024], replicated, may hold values from -3 to 3
- norm_gains: float32 [2, 2, 2, 1024], P('section'), may hold values from 0.1 to 1.9
- filters: float32 [2, 2, 2, 112, 1024], P('section', None, None, None, 'lon'), may hold values from -5 to 5
- w_in: bfloat16 [2, 2, 1024, 4096], P('section', None, 'lat'), may hold values from -0.1875 to 0.1875
- w_out: bfloat16 [2, 2, 1024, 4096], P('section', None, 'lat'), may hold values from -0.09375 to 0.09375
Outputs:
- first_pass: bfloat16 [2, 112, 360, 1024], P('section', 'lat', 'lon')
- second_pass: bfloat16 [2, 112, 360, 1024], P('section', 'lat', 'lon')
Inputs may be any that keep to these rules, and one draw needn't show every extreme that they name: `lmax`: some section keeps all 112 degrees in every draw. `mmax`: some section keeps all 96 wavenumbers in every draw.
All inputs are finite; a program needn't handle non-finite values.
Results may differ from a plain program's by a relative error of at most 0.01.
Values may be sent and summed in bfloat16 or wider, within the bound.
No kernel may reach another device: no remote copies, remote signals or barrier semaphores. Data moves between devices by JAX's collectives and lax.ppermute only.
A program may use at most 384 MiB of HBM per device.

v0:
```python
import math
import jax
import jax.numpy as jnp
from jax import lax
from jax.sharding import PartitionSpec as P

MM = 96


def passed_along(value, axis, steps):
    count = lax.axis_size(axis)
    leading, last = (max(0, -steps), min(count, count - steps))
    return lax.ppermute(value, axis, [(source, source + steps) for source in range(leading, last)])


def legendre_table(orders, n_rows, n_degrees):
    rows = jnp.arange(n_rows, dtype=jnp.float32)
    theta = math.pi * (rows + 0.5) / n_rows
    cosine = jnp.cos(theta)
    sine = jnp.sin(theta)
    order = orders[:, None]
    log_start = (
        0.5 * jnp.log((2.0 * order + 1.0) / (4.0 * math.pi))
        + jax.scipy.special.gammaln(order + 0.5)
        - jax.scipy.special.gammaln(0.5)
        - jax.scipy.special.gammaln(order + 1.0)
        + order * jnp.log(sine)[None, :]
    )
    start = jnp.exp(log_start)

    def advance(carry, degree):
        last, before = carry
        level = degree.astype(jnp.float32)
        coef_a = jnp.sqrt(
            jnp.maximum(4.0 * level * level - 1.0, 1.0)
            / jnp.maximum(level * level - order * order, 1.0)
        )
        coef_b = jnp.sqrt(
            jnp.maximum((level - 1.0) ** 2 - order * order, 0.0)
            / jnp.maximum(4.0 * (level - 1.0) ** 2 - 1.0, 1.0)
        )
        general = coef_a * (cosine[None, :] * last - coef_b * before)
        fresh_row = jnp.where(
            level < order, jnp.zeros_like(start), jnp.where(level == order, start, general)
        )
        return ((fresh_row, last), fresh_row)

    _, table = lax.scan(
        advance,
        (jnp.zeros_like(start), jnp.zeros_like(start)),
        jnp.arange(n_degrees, dtype=jnp.int32),
    )
    quad = 2.0 * math.pi * (math.pi / n_rows) * sine
    return (table, table * quad[None, None, :])


def fourier_tables(n_lon):
    columns = jnp.arange(n_lon, dtype=jnp.int32)
    orders = jnp.arange(MM, dtype=jnp.int32)
    phase = 2.0 * math.pi * (columns[:, None] * orders[None, :] % n_lon).astype(jnp.float32) / n_lon
    cos_fwd = jnp.cos(phase) / n_lon
    sin_fwd = -jnp.sin(phase) / n_lon
    weight = jnp.where(orders == 0, 1.0, 2.0).astype(jnp.float32)[:, None]
    inverse = jnp.stack([weight * jnp.cos(phase).T, -weight * jnp.sin(phase).T], 0)
    return (cos_fwd, sin_fwd, inverse)


def layer_norm(values, gain):
    center = values - jnp.mean(values, axis=-1, keepdims=True)
    spread = jnp.mean(center * center, axis=-1, keepdims=True)
    return center * lax.rsqrt(spread + 1e-05) * gain


def pick(stack, index):
    return lax.dynamic_index_in_dim(stack, index, 0, keepdims=False)


def local(state, fresh, cutoff, plan, lmax, mmax, cutoff_table, norm_gains, filters, w_in, w_out):
    highest = lax.Precision.HIGHEST
    section_idx = lax.axis_index("section")
    lat_idx = lax.axis_index("lat")
    n_section = lax.axis_size("section")
    n_lat = lax.axis_size("lat")
    n_lon = lax.axis_size("lon")
    n_rows, n_cols, width = fresh.shape
    n_degrees = filters.shape[3]
    all_rows = n_rows * n_lat
    all_cols = n_cols * n_lon
    m_local = MM // n_lat
    m_global = lat_idx * m_local + jnp.arange(m_local, dtype=jnp.int32)
    plain, weighted = legendre_table(m_global.astype(jnp.float32), all_rows, n_degrees)
    cos_fwd, sin_fwd, inverse = fourier_tables(all_cols)
    l_max = pick(lmax, section_idx)
    m_max = pick(mmax, section_idx)
    keep = (
        (jnp.arange(n_degrees, dtype=jnp.int32) < l_max)[:, None] & (m_global < m_max)[None, :]
    ).astype(jnp.float32)[:, :, None]

    def run_block(tokens, tick):
        block_idx = pick(plan[tick], section_idx)
        cut = pick(cutoff, tick - section_idx + n_section - 1)
        gains = pick(norm_gains[0], block_idx)
        filt = pick(filters[0], block_idx)
        weight_in = pick(w_in[0], block_idx)
        weight_out = pick(w_out[0], block_idx)
        onehot = (jnp.arange(cutoff_table.shape[0], dtype=jnp.int32) == cut).astype(jnp.float32)
        embed = jnp.dot(onehot, cutoff_table, precision=highest)
        base = tokens.astype(jnp.float32) + embed
        normed = layer_norm(base, gains[0]).astype(jnp.bfloat16)
        by_lon = lax.all_to_all(normed, "lon", split_axis=2, concat_axis=1, tiled=True)
        wide = by_lon.astype(jnp.float32)
        real_part = jnp.einsum("jkc,km->jmc", wide, cos_fwd, precision=highest)
        imag_part = jnp.einsum("jkc,km->jmc", wide, sin_fwd, precision=highest)
        spectrum = jnp.stack([real_part, imag_part], 1).astype(jnp.bfloat16)
        by_mode = lax.all_to_all(spectrum, "lat", split_axis=2, concat_axis=0, tiled=True)
        coeff = jnp.einsum(
            "lmj,jrmc->rlmc", weighted, by_mode.astype(jnp.float32), precision=highest
        )
        filt_re = filt[0][:, None, :]
        filt_im = filt[1][:, None, :]
        out_re = keep * (coeff[0] * filt_re - coeff[1] * filt_im)
        out_im = keep * (coeff[0] * filt_im + coeff[1] * filt_re)
        synthesis = jnp.einsum(
            "lmj,rlmc->jrmc", plain, jnp.stack([out_re, out_im], 0), precision=highest
        ).astype(jnp.bfloat16)
        by_row = lax.all_to_all(synthesis, "lat", split_axis=0, concat_axis=2, tiled=True)
        spectral = jnp.einsum(
            "jrmc,rmk->jkc", by_row.astype(jnp.float32), inverse, precision=highest
        ).astype(jnp.bfloat16)
        spectral = lax.all_to_all(spectral, "lon", split_axis=1, concat_axis=2, tiled=True)
        mixed = base + spectral.astype(jnp.float32)
        normed_two = layer_norm(mixed, gains[1]).astype(jnp.bfloat16)
        flat = normed_two.reshape(n_rows * n_cols, width)
        before_act = jnp.dot(
            flat,
            lax.all_gather(weight_in, "lat", axis=0, tiled=True),
            preferred_element_type=jnp.float32,
        )
        hidden = jax.nn.gelu(before_act).astype(jnp.bfloat16)
        projected = lax.dot_general(
            hidden,
            lax.all_gather(weight_out, "lat", axis=0, tiled=True),
            (((1,), (1,)), ((), ())),
            preferred_element_type=jnp.float32,
        )
        result = mixed + projected.reshape(mixed.shape)
        return result.astype(jnp.bfloat16)

    first_out = run_block(state[0], 0)
    handed = passed_along(first_out, "section", 1)
    entering = jnp.where(section_idx == 0, fresh, handed)
    second_out = run_block(entering, 1)
    return (first_out[None], second_out[None])


def solution(mesh):
    return jax.shard_map(
        local,
        mesh=mesh,
        in_specs=(
            P("section", "lat", "lon", None),
            P("lat", "lon", None),
            P(),
            P(),
            P(),
            P(),
            P(),
            P("section", None, None, None),
            P("section", None, None, None, "lon"),
            P("section", None, "lat", None),
            P("section", None, "lat", None),
        ),
        out_specs=(P("section", "lat", "lon", None), P("section", "lat", "lon", None)),
        check_vma=False,
    )
```

profile of v0, /device:TPU:0, one launch (start us, length us, event | category | flops | bytes accessed | tf_op | source)
XLA Modules:
  0.0 1451.1 jit_solution(14158678115372856451)
XLA Ops:
  28.4 12.0 copy.147
  51.6 88.3 %all-to-all-done = bf16[28,90,1024]{1,0,2:T(8,128)(2,1)} async-done(((bf16[28,90,1024]{1,0,2:T(8,128)(2,1)}), bf16[28,90,1024]{1,0,2:T(8,128)(2,1)}, u32[]{:S(2)}, u32[]{:S(2)}) %all-to-all-start) | async-done | bytes 5160992 | tf_op jit(solution)/shard_map/all_to_all | solution.py:110
  139.9 14.5 copy.148
  183.4 162.5 %while.20 = (s32[]{:T(128)}, f32[24,112]{1,0:T(8,128)S(1)}, f32[24,112]{1,0:T(8,128)S(1)}, f32[112,24,112]{2,1,0:T(8,128)S(1)}, s32[112]{0:T(128)S(1)}, /*index=...) while((s32[]{:T(128)}, f32[24,112]{1,0:T(8,128)S(1)}, ...), condition=%wide.region_3.4_spmd.clone.clone.clone, body=%wide.region_2.3_spmd.clone.clone.clone.sunk | while | flops 24742 | bytes 66539 | solution.py:48
  379.5 128.0 %all-to-all-done.2 = bf16[112,2,24,256]{3,1,2,0:T(2,128)(2,1)S(1)} async-done(((bf16[112,2,24,256]{3,1,2,0:T(2,128)(2,1)}), bf16[112,2,24,256]{3,1,2,0:T(2,128)(2,1)S(1)}, u32[]{:S(2)}, u32[]{:S(2)}) %all-to-all-start.2) | async-done | bytes 2752544 | tf_op jit(solution)/shard_map/all_to_all | solution.py:126
  530.4 58.2 %all-to-all-done.3 = bf16[28,360,256]{2,0,1:T(8,128)(2,1)} async-done(((bf16[28,360,256]{2,0,1:T(8,128)(2,1)}), bf16[28,360,256]{2,0,1:T(8,128)(2,1)}, u32[]{:S(2)}, u32[]{:S(2)}) %all-to-all-start.3) | async-done | bytes 5160992 | tf_op jit(solution)/shard_map/all_to_all | solution.py:130
  598.1 11.6 reshape.645
  609.7 14.5 copy.160
  624.2 14.0 reshape.643
  653.7 10.4 copy.191
  664.1 38.2 %fusion.16.clone.4 = bf16[2520,4096]{1,0:T(8,128)(2,1)} fusion(bf16[1,1,1024,4096]{3,2,1,0:T(8,128)(2,1)} %all-gather.9.cloned.1.call-done, f32[2520,1024]{1,0:T(8,128)} %bitcast.198, f32[2520,1024]{1,0:T(8,128)} %reshape.641, f32[1024]{0:T(1024)S(1)} %bitcast.218, f32[2520]{0:T(1024)S(1)} %rsqrt.37, f32[2520]{0:T(1024)S(1)} %div.110, ...), kind=kOutput, calls=%fused_computation.24.clone.clone.clone.1 | convolution fusion | flops 21247672320 | bytes 49704640 | tf_op jit(solution)/shard_map/dot_general | solution.py:134
  702.3 28.7 %fusion.34 = f32[2520,1024]{1,0:T(8,128)} fusion(bf16[1,1,1024,4096]{3,2,1,0:T(8,128)(2,1)} %all-gather.11.cloned.1.call-done, bf16[2520,4096]{1,0:T(8,128)(2,1)} %fusion.16.clone.4), kind=kOutput, calls=%fused_computation.56 | convolution fusion | flops 21139292160 | bytes 39354368 | tf_op jit(solution)/shard_map/dot_general | solution.py:140
  731.0 11.1 reshape.636
  742.0 12.8 add_convert_fusion.1
  761.3 114.8 %collective-permute-done = bf16[28,90,1024]{2,1,0:T(8,128)(2,1)} collective-permute-done((bf16[28,90,1024]{2,1,0:T(8,128)(2,1)}, bf16[28,90,1024]{2,1,0:T(8,128)(2,1)}, u32[]{:S(2)}, u32[]{:S(2)}) %collective-permute-start) | collective-permute-done | bytes 5160992 | tf_op jit(solution)/shard_map/ppermute | solution.py:13
  887.1 12.0 copy.163
  905.5 92.4 %all-to-all-done.4 = bf16[28,90,1024]{1,0,2:T(8,128)(2,1)} async-done(((bf16[28,90,1024]{1,0,2:T(8,128)(2,1)}), bf16[28,90,1024]{1,0,2:T(8,128)(2,1)}, u32[]{:S(2)}, u32[]{:S(2)}) %all-to-all-start.4) | async-done | bytes 5160992 | tf_op jit(solution)/shard_map/all_to_all | solution.py:110
  997.9 14.9 %copy.164 = bf16[28,90,4,256]{3,1,2,0:T(8,128)(2,1)} copy(bf16[28,90,4,256]{1,0,3,2:T(8,128)(2,1)} %bitcast.41) | data formatting | bytes 10321920 | tf_op jit(solution)/shard_map/all_to_all | solution.py:110
  1034.3 80.7 %all_to_all.126 = bf16[28,2,96,256]{3,1,0,2:T(2,128)(2,1)S(1)} all-to-all(bf16[28,2,96,256]{3,1,0,2:T(2,128)(2,1)S(1)} %copy.165), channel_id=1, replica_groups=mesh['section'=2,'lat'=4,'lon'=4] {'lat'}, dimensions={2} | all-to-all | bytes 5505024 | tf_op jit(solution)/shard_map/all_to_all | solution.py:115
  1128.9 64.8 %all_to_all.127 = bf16[112,2,24,256]{3,1,2,0:T(2,128)(2,1)S(1)} all-to-all(bf16[112,2,24,256]{3,1,2,0:T(2,128)(2,1)S(1)} %copy.171), channel_id=1, replica_groups=mesh['section'=2,'lat'=4,'lon'=4] {'lat'}, dimensions={0} | all-to-all | bytes 5505024 | tf_op jit(solution)/shard_map/all_to_all | solution.py:126
  1209.0 10.9 reshape.635
  1219.9 13.8 reshape.640
  1233.7 12.9 add_convert_fusion.2
  1246.6 28.2 %all-to-all-done.7 = bf16[28,360,256]{2,0,1:T(8,128)(2,1)} async-done(((bf16[28,360,256]{2,0,1:T(8,128)(2,1)}), bf16[28,360,256]{2,0,1:T(8,128)(2,1)}, u32[]{:S(2)}, u32[]{:S(2)}) %all-to-all-start.7) | async-done | bytes 5160992 | tf_op jit(solution)/shard_map/all_to_all | solution.py:130
  1274.9 9.6 copy_convert_fusion
  1284.5 11.7 reshape.648
  1296.2 14.5 %copy.176 = f32[28,90,4,256]{3,2,1,0:T(4,128)} copy(f32[28,90,4,256]{3,1,2,0:T(8,128)} %bitcast.187) | data formatting | bytes 20643840 | tf_op jit(solution)/shard_map/convert_element_type | solution.py:131
  1310.7 14.0 reshape.644
  1356.6 35.3 %fusion.24.clone.4 = bf16[2520,4096]{1,0:T(8,128)(2,1)} fusion(bf16[2520,1024]{1,0:T(8,128)(2,1)} %reshape.637, bf16[1,1,1024,4096]{3,2,1,0:T(8,128)(2,1)} %all-gather.13.cloned.1.call-done), kind=kOutput, calls=%fused_computation.32.clone.clone.clone.1 | convolution fusion | flops 21232189440 | bytes 34193408 | tf_op jit(solution)/shard_map/dot_general | solution.py:134
  1391.9 28.8 %fusion.30 = f32[2520,1024]{1,0:T(8,128)} fusion(bf16[1,1,1024,4096]{3,2,1,0:T(8,128)(2,1)} %all-gather.15.cloned.1.call-done, bf16[2520,4096]{1,0:T(8,128)(2,1)} %fusion.24.clone.4), kind=kOutput, calls=%fused_computation.53 | convolution fusion | flops 21139292160 | bytes 39354368 | tf_op jit(solution)/shard_map/dot_general | solution.py:140
  1420.7 10.8 reshape.638
  1431.5 12.8 fusion.38
  (716 shorter events, 329.0 us)
Async XLA Ops:
  7.2 5.5 copy-start
  11.1 6.3 copy-start.2
  13.6 7.2 copy-start.22
  40.4 99.5 %all-to-all-start = ((bf16[28,90,1024]{1,0,2:T(8,128)(2,1)}), bf16[28,90,1024]{1,0,2:T(8,128)(2,1)}, u32[]{:S(2)}, u32[]{:S(2)}) async-start(bf16[28,90,1024]{1,0,2:T(8,128)(2,1)} %copy.147), calls=%async_computation | async-start | bytes 16777216 | tf_op jit(solution)/shard_map/all_to_all | solution.py:110
  46.0 618.1 %all-gather.9.cloned.1.call-start = ((), (), s32[]{:S(2)}) async-start(), calls=%async_computation.8 | async-start | bytes 10485760 | tf_op jit(solution)/shard_map/all_gather | solution.py:136
  162.6 6.3 copy-start.4
  173.1 172.8 %copy-start.23 = (s32[2]{0:T(128)S(1)}, s32[2]{0:T(128)}, u32[]{:S(2)}) copy-start(s32[2]{0:T(128)} %param.18) | copy-start | bytes 28
  173.1 173.5 %copy-start.24 = (s32[2]{0:T(128)S(1)}, s32[2]{0:T(128)}, u32[]{:S(2)}) copy-start(s32[2]{0:T(128)} %param.17) | copy-start | bytes 28
  177.4 171.6 %copy-start.17 = (f32[1,2,2,112,256]{4,3,2,1,0:T(8,128)S(1)}, f32[1,2,2,112,256]{4,3,2,1,0:T(8,128)}, u32[]{:S(2)}) copy-start(f32[1,2,2,112,256]{4,3,2,1,0:T(8,128)} %param.21) | copy-start | bytes 1376260
  177.4 173.9 %all-to-all-start.1 = ((bf16[28,2,96,256]{3,1,0,2:T(2,128)(2,1)}), bf16[28,2,96,256]{3,1,0,2:T(2,128)(2,1)}, u32[]{:S(2)}, u32[]{:S(2)}) async-start(bf16[28,2,96,256]{3,1,0,2:T(2,128)(2,1)} %copy.149), calls=%async_computation.1 | async-start | bytes 5505024 | tf_op jit(solution)/shard_map/all_to_all | solution.py:115
  345.9 3.9 copy-start.10
  347.7 11.6 copy-start.6
  349.9 8.5 copy-start.18
  351.3 3.2 copy-start.8
  368.2 139.3 %all-to-all-start.2 = ((bf16[112,2,24,256]{3,1,2,0:T(2,128)(2,1)}), bf16[112,2,24,256]{3,1,2,0:T(2,128)(2,1)S(1)}, u32[]{:S(2)}, u32[]{:S(2)}) async-start(bf16[112,2,24,256]{3,1,2,0:T(2,128)(2,1)} %copy.155), calls=%async_computation.2 | async-start | bytes 5505024 | tf_op jit(solution)/shard_map/all_to_all | solution.py:126
  373.3 329.0 %all-gather.11.cloned.1.call-start = ((), (), s32[]{:S(2)}) async-start(), calls=%async_computation.9 | async-start | bytes 10485760 | tf_op jit(solution)/shard_map/all_gather | solution.py:142
  378.9 129.4 %copy-start.11 = (f32[1,96,360]{2,1,0:T(8,128)}, f32[1,96,360]{2,1,0:T(8,128)S(1)}, u32[]{:S(2)}) copy-start(f32[1,96,360]{2,1,0:T(8,128)S(1)} %cosine_multiply_fusion.1) | copy-start | bytes 414724
  379.5 128.8 %copy-start.13 = (f32[1,96,360]{2,1,0:T(8,128)}, f32[1,96,360]{2,1,0:T(8,128)S(1)}, u32[]{:S(2)}) copy-start(f32[1,96,360]{2,1,0:T(8,128)S(1)} %sine_multiply_fusion) | copy-start | bytes 414724
  516.8 71.8 %all-to-all-start.3 = ((bf16[28,360,256]{2,0,1:T(8,128)(2,1)}), bf16[28,360,256]{2,0,1:T(8,128)(2,1)}, u32[]{:S(2)}, u32[]{:S(2)}) async-start(bf16[28,360,256]{2,0,1:T(8,128)(2,1)} %copy.158), calls=%async_computation.3 | async-start | bytes 11796480 | tf_op jit(solution)/shard_map/all_to_all | solution.py:130
  754.8 121.3 %collective-permute-start = (bf16[28,90,1024]{2,1,0:T(8,128)(2,1)}, bf16[28,90,1024]{2,1,0:T(8,128)(2,1)}, u32[]{:S(2)}, u32[]{:S(2)}) collective-permute-start(bf16[28,90,1024]{2,1,0:T(8,128)(2,1)} %add_convert_fusion.1), channel_id=1, source_target_pairs={{0,16},{1,17},{2,18},{3,19},{4,20},{5,21},{6,22},{7,23},{8,24},{9,... | collective-permute-start | bytes 15482888 | tf_op jit(solution)/shard_map/ppermute | solution.py:13
  899.1 98.8 %all-to-all-start.4 = ((bf16[28,90,1024]{1,0,2:T(8,128)(2,1)}), bf16[28,90,1024]{1,0,2:T(8,128)(2,1)}, u32[]{:S(2)}, u32[]{:S(2)}) async-start(bf16[28,90,1024]{1,0,2:T(8,128)(2,1)} %copy.163), calls=%async_computation.4 | async-start | bytes 16777216 | tf_op jit(solution)/shard_map/all_to_all | solution.py:110
  904.7 451.9 %all-gather.13.cloned.1.call-start = ((), (), s32[]{:S(2)}) async-start(), calls=%async_computation.10 | async-start | bytes 10485760 | tf_op jit(solution)/shard_map/all_gather | solution.py:136
  1021.0 6.3 copy-start.5
  1115.9 4.3 copy-start.15
  1115.9 4.3 copy-start.16
  1115.9 4.3 copy-start.19
  1203.1 71.7 %all-to-all-start.7 = ((bf16[28,360,256]{2,0,1:T(8,128)(2,1)}), bf16[28,360,256]{2,0,1:T(8,128)(2,1)}, u32[]{:S(2)}, u32[]{:S(2)}) async-start(bf16[28,360,256]{2,0,1:T(8,128)(2,1)} %copy.174), calls=%async_computation.7 | async-start | bytes 11796480 | tf_op jit(solution)/shard_map/all_to_all | solution.py:130
  1208.4 183.5 %all-gather.15.cloned.1.call-start = ((), (), s32[]{:S(2)}) async-start(), calls=%async_computation.11 | async-start | bytes 10485760 | tf_op jit(solution)/shard_map/all_gather | solution.py:142
  1324.7 15.6 %slice-start = ((s8[5505024]{0:T(1024)(128)(4,1)}), s8[4194304]{0:T(1024)(128)(4,1)S(1)}, s32[]{:S(2)}) async-start(s8[5505024]{0:T(1024)(128)(4,1)} %bitcast.183), calls=%async_computation.12 | async-start | bytes 8388608
  1332.1 8.2 slice-start.1
  1332.1 8.2 copy-start.20
  1431.5 12.8 copy-start.1
  (6 other events, 9.5 us)
Sparse Core Ops, SparseCore 0:
  51.5 178.2 all-gather.8
  378.4 191.6 all-gather.10
  907.1 178.0 all-gather.12
  1210.5 149.1 all-gather.14
where the time goes:
time: 1460 us; the launch traced here: 1450 us
  waiting for transfers between devices  511 us (35%)
  local copies, waits for them, and re-layouts  333 us (23%)
  matrix products  180 us (12%)
  blocking collectives  146 us (10%)
  other arithmetic  145 us (10%)
  loops' own time  78.3 us (5%)
  starting transfers between devices  39.6 us (3%)
  between operations  18.6 us (1%)
    all_to_all x2, waiting for transfers between devices, run_block(): lax.all_to_all(normed, 'lon', split_axis=2, concat_axis=1, tiled=True)  181 us
    all_to_all x1, waiting for transfers between devices, run_block(): lax.all_to_all(synthesis, 'lat', split_axis=0, concat_axis=2, tiled=True)  128 us
    ppermute x1, waiting for transfers between devices, passed_along(): lax.ppermute(value, axis, [(source, source + steps) for source in range(l...  115 us
    convert_element_type x7, local copies, waits for them, and re-layouts, run_block(): mixed = base + spectral.astype(jnp.float32)  94 us
    all_to_all x2, waiting for transfers between devices, run_block(): lax.all_to_all(spectral, 'lon', split_axis=1, concat_axis=2, tiled=True)  86.5 us
    all_to_all x1, blocking collectives, run_block(): lax.all_to_all(spectrum, 'lat', split_axis=2, concat_axis=0, tiled=True)  80.7 us
    another operation x1, loops' own time, legendre_table(): lax.scan(advance, (jnp.zeros_like(start), jnp.zeros_like(start)), jnp.ara...  78.3 us
    dot_general x2, matrix products, run_block(): jnp.dot(flat, lax.all_gather(weight_in, 'lat', axis=0, tiled=True), prefe...  73.5 us
  transfers between devices with their start and end apart: 11, of which 6 were waited for; matrix products, arithmetic and copies ran while one was open for 33% of the time, Pallas kernels for 0%

commit v1 on v0

--- a/solution.py
+++ b/solution.py
@@ -5,6 +5,12 @@
 from jax.sharding import PartitionSpec as P
 
 MM = 96
+
+
+def exchange_blocks(block, mesh_axis, split, join):
+    parts = jnp.split(block, lax.axis_size(mesh_axis), axis=split)
+    incoming = lax.all_to_all(jnp.stack(parts), mesh_axis, 0, 0)
+    return jnp.concatenate(incoming, axis=join)
 
 
 def passed_along(value, axis, steps):
@@ -127,7 +133,7 @@
         spectral = jnp.einsum(
             "jrmc,rmk->jkc", by_row.astype(jnp.float32), inverse, precision=highest
         ).astype(jnp.bfloat16)
-        spectral = lax.all_to_all(spectral, "lon", split_axis=1, concat_axis=2, tiled=True)
+        spectral = exchange_blocks(spectral, "lon", 1, 2)
         mixed = base + spectral.astype(jnp.float32)
         normed_two = layer_norm(mixed, gains[1]).astype(jnp.bfloat16)
         flat = normed_two.reshape(n_rows * n_cols, width)

time: 1460 us -> 1420 us (0.973)
  local copies, waits for them, and re-layouts: 333 us -> 300 us
    convert_element_type x7 -> x5, local copies, waits for them, and re-layouts: 94 us -> 65.1 us  [run_block(): mixed = base + spectral.astype(jnp.float32)]
  transfers between devices with their start and end apart: 11 -> 11, of which waited for: 6 -> 6; matrix products, arithmetic and copies ran while one was open for 33% -> 32% of each run, Pallas kernels for 0% -> 0%
where the time goes in v1:
time: 1420 us; the launch traced here: 1410 us
  waiting for transfers between devices  503 us (35%)
  local copies, waits for them, and re-layouts  300 us (21%)
  matrix products  180 us (13%)
  blocking collectives  146 us (10%)
  other arithmetic  141 us (10%)
  loops' own time  78.3 us (6%)
  starting transfers between devices  39.3 us (3%)
  between operations  18.7 us (1%)
    all_to_all x2, waiting for transfers between devices, run_block(): lax.all_to_all(normed, 'lon', split_axis=2, concat_axis=1, tiled=True)  181 us
    all_to_all x1, waiting for transfers between devices, run_block(): lax.all_to_all(synthesis, 'lat', split_axis=0, concat_axis=2, tiled=True)  128 us
    ppermute x1, waiting for transfers between devices, passed_along(): lax.ppermute(value, axis, [(source, source + steps) for source in range(l...  115 us
    all_to_all x1, blocking collectives, run_block(): lax.all_to_all(spectrum, 'lat', split_axis=2, concat_axis=0, tiled=True)  80.9 us
    another operation x1, loops' own time, legendre_table(): lax.scan(advance, (jnp.zeros_like(start), jnp.zeros_like(start)), jnp.ara...  78.3 us
    all_to_all x2, waiting for transfers between devices, exchange_blocks(): incoming = lax.all_to_all(jnp.stack(parts), mesh_axis, 0, 0)  77.9 us
    dot_general x2, matrix products, run_block(): jnp.dot(flat, lax.all_gather(weight_in, 'lat', axis=0, tiled=True), prefe...  73.3 us
    dynamic_slice x112, local copies, waits for them, and re-layouts, legendre_table(): lax.scan(advance, (jnp.zeros_like(start), jnp.zeros_like(start)), jnp.ara...  66 us
  transfers between devices with their start and end apart: 11, of which 6 were waited for; matrix products, arithmetic and copies ran while one was open for 32% of the time, Pallas kernels for 0%

profile of v1, /device:TPU:0, one launch (start us, length us, event | category | flops | bytes accessed | tf_op | source)
XLA Modules:
  0.0 1406.3 jit_solution(3135311183727737770)
XLA Ops:
  28.3 12.0 copy.89
  51.1 88.8 %all-to-all-done = bf16[28,90,1024]{1,0,2:T(8,128)(2,1)} async-done(((bf16[28,90,1024]{1,0,2:T(8,128)(2,1)}), bf16[28,90,1024]{1,0,2:T(8,128)(2,1)}, u32[]{:S(2)}, u32[]{:S(2)}) %all-to-all-start) | async-done | bytes 5160992 | tf_op jit(solution)/shard_map/all_to_all | solution.py:116
  139.9 14.5 %copy.90 = bf16[28,90,4,256]{3,1,2,0:T(8,128)(2,1)} copy(bf16[28,90,4,256]{1,0,3,2:T(8,128)(2,1)} %bitcast.10) | data formatting | bytes 10321920 | tf_op jit(solution)/shard_map/all_to_all | solution.py:116
  154.3 8.3 all_to_all.87
  183.4 162.5 %while.20 = (s32[]{:T(128)}, f32[24,112]{1,0:T(8,128)S(1)}, f32[24,112]{1,0:T(8,128)S(1)}, f32[112,24,112]{2,1,0:T(8,128)S(1)}, s32[112]{0:T(128)S(1)}, /*index=...) while((s32[]{:T(128)}, f32[24,112]{1,0:T(8,128)S(1)}, ...), condition=%wide.region_3.4_spmd.clone.clone.clone, body=%wide.region_2.3_spmd.clone.clone.clone.sunk | while | flops 24742 | bytes 66539 | solution.py:54
  379.7 127.7 %all-to-all-done.2 = bf16[112,2,24,256]{3,1,2,0:T(2,128)(2,1)S(1)} async-done(((bf16[112,2,24,256]{3,1,2,0:T(2,128)(2,1)}), bf16[112,2,24,256]{3,1,2,0:T(2,128)(2,1)S(1)}, u32[]{:S(2)}, u32[]{:S(2)}) %all-to-all-start.2) | async-done | bytes 2752544 | tf_op jit(solution)/shard_map/all_to_all | solution.py:132
  532.2 54.0 %all-to-all-done.3 = bf16[4,28,90,256]{3,2,1,0:T(8,128)(2,1)} async-done(((bf16[4,28,90,256]{3,2,1,0:T(8,128)(2,1)}), bf16[4,28,90,256]{3,2,1,0:T(8,128)(2,1)}, u32[]{:S(2)}, u32[]{:S(2)}) %all-to-all-start.3) | async-done | bytes 5160992 | tf_op jit(solution)/shard_map/all_to_all | solution.py:12
  590.3 12.1 copy.100
  602.3 13.5 reshape.639
  631.4 10.3 copy.129
  641.7 38.2 %fusion.16.clone.4 = bf16[2520,4096]{1,0:T(8,128)(2,1)} fusion(bf16[1,1,1024,4096]{3,2,1,0:T(8,128)(2,1)} %all-gather.9.cloned.1.call-done, f32[2520,1024]{1,0:T(8,128)} %bitcast.214, f32[2520,1024]{1,0:T(8,128)} %reshape.637, f32[1024]{0:T(1024)S(1)} %bitcast.234, f32[2520]{0:T(1024)S(1)} %rsqrt.37, f32[2520]{0:T(1024)S(1)} %div.110, ...), kind=kOutput, calls=%fused_computation.24.clone.clone.clone.1 | convolution fusion | flops 21247672320 | bytes 49704640 | tf_op jit(solution)/shard_map/dot_general | solution.py:140
  679.9 28.6 %fusion.34 = f32[2520,1024]{1,0:T(8,128)} fusion(bf16[1,1,1024,4096]{3,2,1,0:T(8,128)(2,1)} %all-gather.11.cloned.1.call-done, bf16[2520,4096]{1,0:T(8,128)(2,1)} %fusion.16.clone.4), kind=kOutput, calls=%fused_computation.58 | convolution fusion | flops 21139292160 | bytes 39354368 | tf_op jit(solution)/shard_map/dot_general | solution.py:146
  708.5 11.2 reshape.632
  719.7 12.8 add_convert_fusion.1
  739.0 114.7 %collective-permute-done = bf16[28,90,1024]{2,1,0:T(8,128)(2,1)} collective-permute-done((bf16[28,90,1024]{2,1,0:T(8,128)(2,1)}, bf16[28,90,1024]{2,1,0:T(8,128)(2,1)}, u32[]{:S(2)}, u32[]{:S(2)}) %collective-permute-start) | collective-permute-done | bytes 5160992 | tf_op jit(solution)/shard_map/ppermute | solution.py:19
  864.6 12.0 copy.103
  883.0 92.4 %all-to-all-done.4 = bf16[28,90,1024]{1,0,2:T(8,128)(2,1)} async-done(((bf16[28,90,1024]{1,0,2:T(8,128)(2,1)}), bf16[28,90,1024]{1,0,2:T(8,128)(2,1)}, u32[]{:S(2)}, u32[]{:S(2)}) %all-to-all-start.4) | async-done | bytes 5160992 | tf_op jit(solution)/shard_map/all_to_all | solution.py:116
  975.4 14.6 %copy.104 = bf16[28,90,4,256]{3,1,2,0:T(8,128)(2,1)} copy(bf16[28,90,4,256]{1,0,3,2:T(8,128)(2,1)} %bitcast.45) | data formatting | bytes 10321920 | tf_op jit(solution)/shard_map/all_to_all | solution.py:116
  990.0 8.3 all_to_all.100
  1011.6 80.9 %all_to_all.118 = bf16[28,2,96,256]{3,1,0,2:T(2,128)(2,1)S(1)} all-to-all(bf16[28,2,96,256]{3,1,0,2:T(2,128)(2,1)S(1)} %copy.105), channel_id=1, replica_groups=mesh['section'=2,'lat'=4,'lon'=4] {'lat'}, dimensions={2} | all-to-all | bytes 5505024 | tf_op jit(solution)/shard_map/all_to_all | solution.py:121
  1106.4 64.6 %all_to_all.119 = bf16[112,2,24,256]{3,1,2,0:T(2,128)(2,1)S(1)} all-to-all(bf16[112,2,24,256]{3,1,2,0:T(2,128)(2,1)S(1)} %copy.111), channel_id=1, replica_groups=mesh['section'=2,'lat'=4,'lon'=4] {'lat'}, dimensions={0} | all-to-all | bytes 5505024 | tf_op jit(solution)/shard_map/all_to_all | solution.py:132
  1188.1 11.1 reshape.631
  1199.2 13.7 reshape.636
  1212.9 13.0 add_convert_fusion.2
  1225.8 23.9 %all-to-all-done.7 = bf16[4,28,90,256]{3,2,1,0:T(8,128)(2,1)} async-done(((bf16[4,28,90,256]{3,2,1,0:T(8,128)(2,1)}), bf16[4,28,90,256]{3,2,1,0:T(8,128)(2,1)}, u32[]{:S(2)}, u32[]{:S(2)}) %all-to-all-start.7) | async-done | bytes 5160992 | tf_op jit(solution)/shard_map/all_to_all | solution.py:12
  1253.8 12.2 copy.114
  1266.1 13.6 reshape.640
  1295.4 8.5 multiply_convert_fusion
  1311.8 35.2 %fusion.24.clone.4 = bf16[2520,4096]{1,0:T(8,128)(2,1)} fusion(bf16[2520,1024]{1,0:T(8,128)(2,1)} %reshape.633, bf16[1,1,1024,4096]{3,2,1,0:T(8,128)(2,1)} %all-gather.13.cloned.1.call-done), kind=kOutput, calls=%fused_computation.32.clone.clone.clone.1 | convolution fusion | flops 21232189440 | bytes 34193408 | tf_op jit(solution)/shard_map/dot_general | solution.py:140
  1347.0 28.9 %fusion.30 = f32[2520,1024]{1,0:T(8,128)} fusion(bf16[1,1,1024,4096]{3,2,1,0:T(8,128)(2,1)} %all-gather.15.cloned.1.call-done, bf16[2520,4096]{1,0:T(8,128)(2,1)} %fusion.24.clone.4), kind=kOutput, calls=%fused_computation.55 | convolution fusion | flops 21139292160 | bytes 39354368 | tf_op jit(solution)/shard_map/dot_general | solution.py:146
  1375.8 10.8 reshape.634
  1386.7 12.8 fusion.38
  (716 shorter events, 306.1 us)
Async XLA Ops:
  7.2 5.5 copy-start
  11.1 6.2 copy-start.2
  13.6 7.2 copy-start.22
  40.3 99.5 %all-to-all-start = ((bf16[28,90,1024]{1,0,2:T(8,128)(2,1)}), bf16[28,90,1024]{1,0,2:T(8,128)(2,1)}, u32[]{:S(2)}, u32[]{:S(2)}) async-start(bf16[28,90,1024]{1,0,2:T(8,128)(2,1)} %copy.89), calls=%async_computation | async-start | bytes 16777216 | tf_op jit(solution)/shard_map/all_to_all | solution.py:116
  46.0 595.7 %all-gather.9.cloned.1.call-start = ((), (), s32[]{:S(2)}) async-start(), calls=%async_computation.8 | async-start | bytes 10485760 | tf_op jit(solution)/shard_map/all_gather | solution.py:142
  162.6 6.3 copy-start.4
  173.1 172.8 %copy-start.23 = (s32[2]{0:T(128)S(1)}, s32[2]{0:T(128)}, u32[]{:S(2)}) copy-start(s32[2]{0:T(128)} %param.18) | copy-start | bytes 28
  173.1 173.6 %copy-start.24 = (s32[2]{0:T(128)S(1)}, s32[2]{0:T(128)}, u32[]{:S(2)}) copy-start(s32[2]{0:T(128)} %param.17) | copy-start | bytes 28
  177.4 171.7 %copy-start.17 = (f32[1,2,2,112,256]{4,3,2,1,0:T(8,128)S(1)}, f32[1,2,2,112,256]{4,3,2,1,0:T(8,128)}, u32[]{:S(2)}) copy-start(f32[1,2,2,112,256]{4,3,2,1,0:T(8,128)} %param.21) | copy-start | bytes 1376260
  177.4 173.9 %all-to-all-start.1 = ((bf16[28,2,96,256]{3,1,0,2:T(2,128)(2,1)}), bf16[28,2,96,256]{3,1,0,2:T(2,128)(2,1)}, u32[]{:S(2)}, u32[]{:S(2)}) async-start(bf16[28,2,96,256]{3,1,0,2:T(2,128)(2,1)} %copy.91), calls=%async_computation.1 | async-start | bytes 5505024 | tf_op jit(solution)/shard_map/all_to_all | solution.py:121
  345.9 4.0 copy-start.10
  347.7 11.7 copy-start.6
  349.9 8.5 copy-start.18
  351.4 3.2 copy-start.8
  368.2 139.2 %all-to-all-start.2 = ((bf16[112,2,24,256]{3,1,2,0:T(2,128)(2,1)}), bf16[112,2,24,256]{3,1,2,0:T(2,128)(2,1)S(1)}, u32[]{:S(2)}, u32[]{:S(2)}) async-start(bf16[112,2,24,256]{3,1,2,0:T(2,128)(2,1)} %copy.97), calls=%async_computation.2 | async-start | bytes 5505024 | tf_op jit(solution)/shard_map/all_to_all | solution.py:132
  373.3 306.5 %all-gather.11.cloned.1.call-start = ((), (), s32[]{:S(2)}) async-start(), calls=%async_computation.9 | async-start | bytes 10485760 | tf_op jit(solution)/shard_map/all_gather | solution.py:148
  379.1 129.1 %copy-start.11 = (f32[1,96,360]{2,1,0:T(8,128)}, f32[1,96,360]{2,1,0:T(8,128)S(1)}, u32[]{:S(2)}) copy-start(f32[1,96,360]{2,1,0:T(8,128)S(1)} %cosine_multiply_fusion.1) | copy-start | bytes 414724
  379.7 128.5 %copy-start.13 = (f32[1,96,360]{2,1,0:T(8,128)}, f32[1,96,360]{2,1,0:T(8,128)S(1)}, u32[]{:S(2)}) copy-start(f32[1,96,360]{2,1,0:T(8,128)S(1)} %sine_multiply_fusion) | copy-start | bytes 414724
  518.6 67.6 %all-to-all-start.3 = ((bf16[4,28,90,256]{3,2,1,0:T(8,128)(2,1)}), bf16[4,28,90,256]{3,2,1,0:T(8,128)(2,1)}, u32[]{:S(2)}, u32[]{:S(2)}) async-start(bf16[4,28,90,256]{3,2,1,0:T(8,128)(2,1)} %pad_maximum_fusion), calls=%async_computation.3 | async-start | bytes 11010048 | tf_op jit(solution)/shard_map/all_to_all | solution.py:12
  732.4 121.3 %collective-permute-start = (bf16[28,90,1024]{2,1,0:T(8,128)(2,1)}, bf16[28,90,1024]{2,1,0:T(8,128)(2,1)}, u32[]{:S(2)}, u32[]{:S(2)}) collective-permute-start(bf16[28,90,1024]{2,1,0:T(8,128)(2,1)} %add_convert_fusion.1), channel_id=1, source_target_pairs={{0,16},{1,17},{2,18},{3,19},{4,20},{5,21},{6,22},{7,23},{8,24},{9,... | collective-permute-start | bytes 15482888 | tf_op jit(solution)/shard_map/ppermute | solution.py:19
  876.6 98.8 %all-to-all-start.4 = ((bf16[28,90,1024]{1,0,2:T(8,128)(2,1)}), bf16[28,90,1024]{1,0,2:T(8,128)(2,1)}, u32[]{:S(2)}, u32[]{:S(2)}) async-start(bf16[28,90,1024]{1,0,2:T(8,128)(2,1)} %copy.103), calls=%async_computation.4 | async-start | bytes 16777216 | tf_op jit(solution)/shard_map/all_to_all | solution.py:116
  882.3 429.5 %all-gather.13.cloned.1.call-start = ((), (), s32[]{:S(2)}) async-start(), calls=%async_computation.10 | async-start | bytes 10485760 | tf_op jit(solution)/shard_map/all_gather | solution.py:142
  998.3 6.3 copy-start.5
  1093.5 4.3 copy-start.15
  1093.5 4.3 copy-start.16
  1093.5 4.3 copy-start.19
  1182.4 67.4 %all-to-all-start.7 = ((bf16[4,28,90,256]{3,2,1,0:T(8,128)(2,1)}), bf16[4,28,90,256]{3,2,1,0:T(8,128)(2,1)}, u32[]{:S(2)}, u32[]{:S(2)}) async-start(bf16[4,28,90,256]{3,2,1,0:T(8,128)(2,1)} %pad_maximum_fusion.1), calls=%async_computation.7 | async-start | bytes 11010048 | tf_op jit(solution)/shard_map/all_to_all | solution.py:12
  1187.5 159.5 %all-gather.15.cloned.1.call-start = ((), (), s32[]{:S(2)}) async-start(), calls=%async_computation.11 | async-start | bytes 10485760 | tf_op jit(solution)/shard_map/all_gather | solution.py:148
  1279.7 15.7 %slice-start = ((s8[5505024]{0:T(1024)(128)(4,1)}), s8[4194304]{0:T(1024)(128)(4,1)S(1)}, s32[]{:S(2)}) async-start(s8[5505024]{0:T(1024)(128)(4,1)} %bitcast.201), calls=%async_computation.12 | async-start | bytes 8388608
  1287.1 8.2 slice-start.1
  1287.1 8.2 copy-start.20
  1386.7 12.8 copy-start.1
  (6 other events, 9.3 us)
Sparse Core Ops, SparseCore 0:
  51.0 178.0 all-gather.8
  378.6 191.4 all-gather.10
  884.7 178.0 all-gather.12
  1189.6 149.1 all-gather.14
